TPU v7x, 32 devices: a whole 2x2x4 slice. The times are simulated.
32 devices in a mesh: blk: 16 (over z, y, core), col: 2 (over x).
Axes of the slice: x: 2, y: 2, z: 4, core: 2. Of those that a mesh axis runs over, the one named last changes fastest.
Arguments:
- encodings: bfloat16 [8192, 1024], P(('blk', 'col')), may hold values from -8 to 8
- first_weight: bfloat16 [1024, 512], replicated, may hold values from -0.1875 to 0.1875
- second_weight: bfloat16 [512, 32], replicated, may hold values from -0.25 to 0.25
- inv_scale: float32 [32], replicated, may hold values from 0.2 to 0.8
- outputscale: float32 [1], replicated, may hold values from 0.5 to 2
- noise: float32 [1], replicated, may hold values from 0.2 to 2
- rhs: float32 [32, 8192], P('col', 'blk'), may hold values from -12 to 12
Outputs:
- solution: float32 [32, 8192], P('col', 'blk')
- residual: float32 [32, 8192], P('col', 'blk')
All inputs are finite; a program needn't handle non-finite values.
Results may differ from a plain program's by a relative error of at most 0.0079.
Values sent between devices are 32-bit elements; how exact they have to be, the bound alone decides.
A program may use at most 64 MiB of HBM per device.

v0:
```python
import jax
import jax.numpy as jnp
from jax import lax
from jax.sharding import PartitionSpec as P


def square_sums(residual):
    return lax.psum(jnp.sum(residual * residual, axis=1), "blk")


def split_blocks(values, width):
    count = values.shape[1] // width
    return values.reshape(values.shape[0], count, width).transpose(1, 0, 2)


def on_device(encodings, first_weight, second_weight, inv_scale, outputscale, noise, rhs):
    hidden = jnp.maximum(
        jnp.dot(encodings, first_weight, preferred_element_type=jnp.float32), 0.0
    ).astype(jnp.bfloat16)
    features = (
        jnp.einsum("hf,nh->fn", second_weight, hidden, preferred_element_type=jnp.float32)
        * inv_scale[:, None]
    )
    paired = lax.all_gather(features, "col", axis=1, tiled=True)
    shard_width = features.shape[1]
    row_norms = jnp.sum(paired * paired, axis=0)
    kernel_scale = outputscale[0]
    nugget = noise[0]
    residual = rhs
    norm_now = square_sums(residual)
    moving = lax.all_to_all(rhs, "col", split_axis=1, concat_axis=0, tiled=True)
    initial = jnp.zeros((moving.shape[0], paired.shape[1]), jnp.float32)

    def advance(running, blocks):
        feat_block, dir_block = blocks
        cross = lax.dot_general(
            paired, feat_block, (((0,), (0,)), ((), ())), precision=lax.Precision.HIGHEST
        )
        distance = (
            row_norms[:, None] + jnp.sum(feat_block * feat_block, axis=0)[None, :] - 2.0 * cross
        )
        kernel_tile = kernel_scale * jnp.exp(-0.5 * distance)
        added = lax.dot_general(
            dir_block, kernel_tile, (((1,), (1,)), ((), ())), precision=lax.Precision.HIGHEST
        )
        return (running + added, None)

    images = lax.scan(
        advance,
        initial,
        (
            split_blocks(lax.all_gather(features, "blk", axis=1, tiled=True), shard_width),
            split_blocks(lax.all_gather(moving, "blk", axis=1, tiled=True), shard_width),
        ),
    )[0]
    images = lax.psum_scatter(images, "col", scatter_dimension=0, tiled=True)
    images = images + nugget * rhs
    bent = lax.psum(jnp.sum(rhs * images, axis=1), "blk")
    step_size = norm_now / bent
    solution = step_size[:, None] * rhs
    residual = residual - step_size[:, None] * images
    return (solution, residual)


def solution(mesh):
    placed = (P(("blk", "col"), None), P(), P(), P(), P(), P(), P("col", "blk"))
    return jax.shard_map(
        on_device,
        mesh=mesh,
        in_specs=placed,
        out_specs=(P("col", "blk"), P("col", "blk")),
        check_vma=False,
    )
```

profile of v0, /device:TPU:0, one launch (start us, length us, event | category | flops | bytes accessed | tf_op | source)
XLA Modules:
  0.0 143.1 jit_solution(18136698835859300657)
XLA Ops:
  7.2 0.0 copy-start
  7.2 1.5 %copy.27 = f32[2,2,8,256]{3,2,0,1:T(8,128)} copy(f32[2,2,8,256]{3,2,1,0:T(8,128)} %bitcast.64) | data formatting | bytes 65536 | tf_op jit(solution)/shard_map/all_to_all | solution.py:31
  8.6 4.4 %all-to-all-start = ((f32[16,2,256]{2,0,1:T(8,128)}), f32[16,2,256]{2,0,1:T(8,128)S(1)}, u32[]{:S(2)}, u32[]{:S(2)}) async-start(f32[16,2,256]{2,0,1:T(8,128)} %bitcast.45), calls=%async_computation | async-start | bytes 65536 | tf_op jit(solution)/shard_map/all_to_all | solution.py:31
  13.0 1.6 %fusion.12 = f32[32,256]{1,0:T(8,128)S(1)} fusion(bf16[512,32]{0,1:T(8,128)(2,1)S(1)} %copy-done.4, bf16[256,1024]{1,0:T(8,128)(2,1)} %param.9, bf16[1024,512]{1,0:T(8,128)(2,1)S(1)} %copy-done, f32[32]{0:T(128)S(1)} %copy-done.5), kind=kOutput, calls=%fused_computation.18 | convolution fusion | flops 277094400 | bytes 1638528 | tf_op jit(solution)/shard_map/hf,nh->fn/dot_general | solution.py:21
  14.6 4.6 %all_gather.10 = f32[32,512]{1,0:T(8,128)S(1)} all-gather(f32[32,256]{1,0:T(8,128)S(1)} %fusion.12), channel_id=1, replica_groups=mesh['blk'=16,'col'=2] {'col'}, dimensions={1}, use_global_device_ids=true | all-gather | bytes 98304 | tf_op jit(solution)/shard_map/all_gather | solution.py:24
  19.2 23.8 %all_gather.11 = f32[32,4096]{1,0:T(8,128)S(1)} all-gather(f32[32,256]{1,0:T(8,128)S(1)} %fusion.12), channel_id=1, replica_groups=mesh['blk'=16,'col'=2] {'blk'}, dimensions={1}, use_global_device_ids=true | all-gather | bytes 557056 | tf_op jit(solution)/shard_map/all_gather | solution.py:52
  43.1 18.9 %all_gather.9 = f32[32,4096]{1,0:T(8,128)S(1)} all-gather(f32[32,256]{1,0:T(8,128)S(1)} %bitcast.65), channel_id=1, replica_groups=mesh['blk'=16,'col'=2] {'blk'}, dimensions={1}, use_global_device_ids=true | all-gather | bytes 557056 | tf_op jit(solution)/shard_map/all_gather | solution.py:53
  62.0 0.2 copy.21
  62.2 30.2 %while.11 = (s32[]{:T(128)}, f32[32,512]{1,0:T(8,128)S(1)}, f32[16,32,256]{2,0,1:T(8,128)S(1)}, f32[]{:T(128)}, f32[512]{0:T(512)S(1)}, /*index=5*/f32[16,32,256...) while((s32[]{:T(128)}, f32[32,512]{1,0:T(8,128)S(1)}, f32[16,32,256]{2,0,1:T(8,128)S(1)}, ...), condition=%wide.region_5.6_spmd.clone, body=%wide.region_3.5_spmd.clone.sunk | while | flops 101367552 | bytes 1413239 | solution.py:48
  62.2 1.4 fusion.29
  63.6 0.4 convolution_add_fusion.2
  64.1 1.4 fusion.29
  65.5 0.4 convolution_add_fusion.2
  66.0 1.4 fusion.29
  67.4 0.4 convolution_add_fusion.2
  67.9 1.4 fusion.29
  69.3 0.4 convolution_add_fusion.2
  69.7 1.4 fusion.29
  71.2 0.4 convolution_add_fusion.2
  71.6 1.4 fusion.29
  73.0 0.4 convolution_add_fusion.2
  73.5 1.4 fusion.29
  74.9 0.4 convolution_add_fusion.2
  75.4 1.4 fusion.29
  76.8 0.4 convolution_add_fusion.2
  77.3 1.4 fusion.29
  78.7 0.4 convolution_add_fusion.2
  79.2 1.4 fusion.29
  80.6 0.4 convolution_add_fusion.2
  81.1 1.4 fusion.29
  82.5 0.4 convolution_add_fusion.2
  82.9 1.4 fusion.29
  84.4 0.4 convolution_add_fusion.2
  84.8 1.4 fusion.29
  86.3 0.4 convolution_add_fusion.2
  86.7 1.4 fusion.29
  88.1 0.4 convolution_add_fusion.2
  88.6 1.4 fusion.29
  90.0 0.4 convolution_add_fusion.2
  90.5 1.4 fusion.29
  91.9 0.4 convolution_add_fusion.2
  92.3 0.0 copy-start.2
  92.4 0.6 copy-done.1
  93.0 0.0 reduce-scatter.2.cloned.1.call-update
  93.6 8.3 %reduce-scatter.2.cloned.1.call-done = f32[16,512]{1,0:T(8,128)} async-done(((f32[32,512]{1,0:T(8,128)}), f32[16,512]{1,0:T(8,128)}) %reduce-scatter.2.cloned.1.call-update) | async-done | bytes 32784 | tf_op jit(solution)/shard_map/reduce_scatter | solution.py:56
  102.0 0.9 multiply_reduce_fusion.1
  102.9 32.6 %all-reduce = (f32[16]{0:T(128)S(1)}, f32[16]{0:T(128)S(1)}) all-reduce(f32[16]{0:T(128)S(1)} %get-tuple-element.86, f32[16]{0:T(128)S(1)} %get-tuple-element.85), channel_id=1, replica_groups=mesh['blk'=16,'col'=2] {'blk'}, use_global_device_ids=true, to_apply=%region_1.0 | all-reduce | flops 32 | bytes 256 | tf_op jit(solution)/shard_map/psum | solution.py:8
  135.5 0.7 multiply_subtract_fusion
  (47 shorter events, 1.1 us)
Async XLA Ops:
  7.2 5.9 %copy-start = (bf16[1024,512]{1,0:T(8,128)(2,1)S(1)}, bf16[1024,512]{1,0:T(8,128)(2,1)}, u32[]{:S(2)}) copy-start(bf16[1024,512]{1,0:T(8,128)(2,1)} %param.10) | copy-start | bytes 3145732
  8.6 4.4 %copy-start.4 = (bf16[512,32]{0,1:T(8,128)(2,1)S(1)}, bf16[512,32]{0,1:T(8,128)(2,1)}, u32[]{:S(2)}) copy-start(bf16[512,32]{0,1:T(8,128)(2,1)} %param.11) | copy-start | bytes 98308
  8.6 4.4 %copy-start.5 = (f32[32]{0:T(128)S(1)}, f32[32]{0:T(128)}, u32[]{:S(2)}) copy-start(f32[32]{0:T(128)} %param.12) | copy-start | bytes 388
  8.6 34.5 %all-to-all-start = ((f32[16,2,256]{2,0,1:T(8,128)}), f32[16,2,256]{2,0,1:T(8,128)S(1)}, u32[]{:S(2)}, u32[]{:S(2)}) async-start(f32[16,2,256]{2,0,1:T(8,128)} %bitcast.45), calls=%async_computation | async-start | bytes 65536 | tf_op jit(solution)/shard_map/all_to_all | solution.py:31
  13.0 89.0 %reduce-scatter.2.cloned.1.call-start = ((), (), s32[]{:S(2)}) async-start(), calls=%async_computation.2 | async-start | bytes 98304 | tf_op jit(solution)/shard_map/reduce_scatter | solution.py:56
  92.3 0.6 copy-start.1
  92.3 9.6 %copy-start.2 = (f32[16,512]{1,0:T(8,128)S(1)}, f32[16,512]{1,0:T(8,128)}, u32[]{:S(2)}) copy-start(f32[16,512]{1,0:T(8,128)} %param.15) | copy-start | bytes 98308
  102.0 33.6 %copy-start.3 = (f32[16,512]{1,0:T(8,128)S(1)}, f32[16,512]{1,0:T(8,128)}, u32[]{:S(2)}) copy-start(f32[16,512]{1,0:T(8,128)} %reduce-scatter.2.cloned.1.call-done) | copy-start | bytes 98308
Sparse Core Ops, SparseCore 0:
  93.1 8.8 reduce-scatter.1
where the time goes:
time: 144 us; the launch traced here: 143 us
  blocking collectives  79.8 us (55%)
  matrix products  30.1 us (21%)
  between operations  14.7 us (10%)
  waiting for transfers between devices  8.35 us (6%)
  starting transfers between devices  4.37 us (3%)
  local copies, waits for them, and re-layouts  2.89 us (2%)
  other arithmetic  2.1 us (1%)
    psum x1, blocking collectives, square_sums(): return lax.psum(jnp.sum(residual * residual, axis=1), 'blk')  32.6 us
    all_gather x1, blocking collectives, on_device(): lax.all_gather(features, 'blk', axis=1, tiled=True)  23.8 us
    dot_general x16, matrix products, advance(): lax.dot_general(paired, feat_block, (((0,), (0,)), ((), ())), precision=l...  21.9 us
    all_gather x1, blocking collectives, on_device(): lax.all_gather(moving, 'blk', axis=1, tiled=True)  18.9 us
    reduce_scatter x1, waiting for transfers between devices, on_device(): images = lax.psum_scatter(images, 'col', scatter_dimension=0, tiled=True)  8.33 us
    dot_general x16, matrix products, advance(): lax.dot_general(dir_block, kernel_tile, (((1,), (1,)), ((), ())), precisi...  6.59 us
    all_gather x1, blocking collectives, on_device(): paired = lax.all_gather(features, 'col', axis=1, tiled=True)  4.59 us
    all_to_all x1, starting transfers between devices, on_device(): moving = lax.all_to_all(rhs, 'col', split_axis=1, concat_axis=0, tiled=True)  4.37 us
  transfers between devices with their start and end apart: 2, of which 1 were waited for; matrix products, arithmetic and copies ran while one was open for 1% of the time, Pallas kernels for 0%

commit v1 on v0

--- a/solution.py
+++ b/solution.py
@@ -2,6 +2,28 @@
 import jax.numpy as jnp
 from jax import lax
 from jax.sharding import PartitionSpec as P
+
+
+def laid_out(pieces, dim):
+    shape = list(pieces.shape[1:])
+    shape[dim] *= pieces.shape[0]
+    return jnp.moveaxis(pieces, 0, dim).reshape(shape)
+
+
+def ring_gather(value, axis, dim):
+    devices = lax.axis_size(axis)
+    pairs = [(i, (i + 1) % devices) for i in range(devices)]
+    back = [(b, a) for a, b in pairs]
+    lower, upper = ([], [])
+    for step in range(devices - 1):
+        if step % 2 == 0:
+            lower.append(lax.ppermute(lower[-1] if lower else value, axis, pairs))
+        else:
+            upper.append(lax.ppermute(upper[-1] if upper else value, axis, back))
+    tiles = jnp.stack([*lower[::-1], value, *upper])
+    shift = lax.axis_index(axis) - len(lower)
+    tiles = tiles[(jnp.arange(devices) - shift) % devices]
+    return laid_out(tiles, dim)
 
 
 def square_sums(residual):
@@ -49,7 +71,7 @@
         advance,
         initial,
         (
-            split_blocks(lax.all_gather(features, "blk", axis=1, tiled=True), shard_width),
+            split_blocks(ring_gather(features, "blk", 1), shard_width),
             split_blocks(lax.all_gather(moving, "blk", axis=1, tiled=True), shard_width),
         ),
     )[0]

time: 144 us -> 167 us (1.16)
  starting transfers between devices: 4.37 us -> 30.8 us
  blocking collectives: 79.8 us -> 56.6 us
  waiting for transfers between devices: 8.35 us -> 26.9 us
    ppermute x0 -> x15, starting transfers between devices: none -> 27.5 us  [the longest x7 27 us: ring_gather(): upper.append(lax.ppermute(upper[-1] if upper else value, axis, back))]
    all_gather x1 -> x0, blocking collectives: 23.8 us -> none  [on_device(): lax.all_gather(features, 'blk', axis=1, tiled=True)]
    ppermute x0 -> x15, waiting for transfers between devices: none -> 16 us  [the longest x8 9.82 us: ring_gather(): lower.append(lax.ppermute(lower[-1] if lower else value, axis, pairs))]
    reduce_scatter x1, waiting for transfers between devices: 8.33 us -> 11 us  [on_device(): images = lax.psum_scatter(images, 'col', scatter_dimension=0, tiled=True)]
  transfers between devices with their start and end apart: 2 -> 17, of which waited for: 1 -> 8; matrix products, arithmetic and copies ran while one was open for 1% -> 1% of each run, Pallas kernels for 0% -> 0%
where the time goes in v1:
time: 167 us; the launch traced here: 166 us
  blocking collectives  56.6 us (34%)
  starting transfers between devices  30.8 us (18%)
  matrix products  30.1 us (18%)
  waiting for transfers between devices  26.9 us (16%)
  between operations  14.9 us (9%)
  local copies, waits for them, and re-layouts  3.87 us (2%)
  other arithmetic  2.12 us (1%)
    psum x1, blocking collectives, square_sums(): return lax.psum(jnp.sum(residual * residual, axis=1), 'blk')  32.6 us
    ppermute x7, starting transfers between devices, ring_gather(): upper.append(lax.ppermute(upper[-1] if upper else value, axis, back))  27 us
    dot_general x16, matrix products, advance(): lax.dot_general(paired, feat_block, (((0,), (0,)), ((), ())), precision=l...  21.9 us
    all_gather x1, blocking collectives, on_device(): lax.all_gather(moving, 'blk', axis=1, tiled=True)  19.4 us
    reduce_scatter x1, waiting for transfers between devices, on_device(): images = lax.psum_scatter(images, 'col', scatter_dimension=0, tiled=True)  11 us
    ppermute x8, waiting for transfers between devices, ring_gather(): lower.append(lax.ppermute(lower[-1] if lower else value, axis, pairs))  9.82 us
    dot_general x16, matrix products, advance(): lax.dot_general(dir_block, kernel_tile, (((1,), (1,)), ((), ())), precisi...  6.59 us
    ppermute x7, waiting for transfers between devices, ring_gather(): upper.append(lax.ppermute(upper[-1] if upper else value, axis, back))  6.13 us
  transfers between devices with their start and end apart: 17, of which 8 were waited for; matrix products, arithmetic and copies ran while one was open for 1% of the time, Pallas kernels for 0%

profile of v1, /device:TPU:0, one launch (start us, length us, event | category | flops | bytes accessed | tf_op | source)
XLA Modules:
  0.0 166.1 jit_solution(5288846960889386372)
XLA Ops:
  7.2 1.2 copy-done
  8.4 1.6 fusion.11
  10.0 0.5 collective-permute-start
  10.6 6.6 %collective-permute-done = f32[32,256]{1,0:T(8,128)S(1)} collective-permute-done((f32[32,256]{1,0:T(8,128)S(1)}, f32[32,256]{1,0:T(8,128)S(1)}, u32[]{:S(2)}, u32[]{:S(2)}) %collective-permute-start) | collective-permute-done | bytes 32800 | tf_op jit(solution)/shard_map/ppermute | solution.py:20
  17.2 4.4 %collective-permute-start.8 = (f32[32,256]{1,0:T(8,128)S(1)}, f32[32,256]{1,0:T(8,128)S(1)}, u32[]{:S(2)}, u32[]{:S(2)}) collective-permute-start(f32[32,256]{1,0:T(8,128)S(1)} %bitcast.91), channel_id=1, source_target_pairs={{2,0},{4,2},{6,4},{8,6},{10,8},{12,10},{14,12},{16,14},{18,16},{20... | collective-permute-start | bytes 98312 | tf_op jit(solution)/shard_map/ppermute | solution.py:22
  21.6 1.6 collective-permute-done.1
  23.2 4.4 %collective-permute-start.9 = (f32[32,256]{1,0:T(8,128)S(1)}, f32[32,256]{1,0:T(8,128)S(1)}, u32[]{:S(2)}, u32[]{:S(2)}) collective-permute-start(f32[32,256]{1,0:T(8,128)S(1)} %collective-permute-done.8), channel_id=1, source_target_pairs={{2,0},{4,2},{6,4},{8,6},{10,8},{12,10},{14,12},{16,14},{18,16},{20... | collective-permute-start | bytes 98312 | tf_op jit(solution)/shard_map/ppermute | solution.py:22
  27.6 1.6 collective-permute-done.2
  29.2 0.6 copy.20
  29.9 3.3 %all-to-all-start = ((f32[16,2,256]{2,0,1:T(8,128)}), f32[16,2,256]{2,0,1:T(8,128)S(1)}, u32[]{:S(2)}, u32[]{:S(2)}) async-start(f32[16,2,256]{2,0,1:T(8,128)} %bitcast.72), calls=%async_computation | async-start | bytes 65536 | tf_op jit(solution)/shard_map/all_to_all | solution.py:53
  33.2 4.6 %all_gather.7 = f32[32,512]{1,0:T(8,128)S(1)} all-gather(f32[32,256]{1,0:T(8,128)S(1)} %bitcast.92), channel_id=1, replica_groups=mesh['blk'=16,'col'=2] {'col'}, dimensions={1}, use_global_device_ids=true | all-gather | bytes 98304 | tf_op jit(solution)/shard_map/all_gather | solution.py:46
  37.8 3.5 %collective-permute-start.10 = (f32[32,256]{1,0:T(8,128)S(1)}, f32[32,256]{1,0:T(8,128)S(1)}, u32[]{:S(2)}, u32[]{:S(2)}) collective-permute-start(f32[32,256]{1,0:T(8,128)S(1)} %collective-permute-done.9), channel_id=1, source_target_pairs={{2,0},{4,2},{6,4},{8,6},{10,8},{12,10},{14,12},{16,14},{18,16},{20... | collective-permute-start | bytes 98312 | tf_op jit(solution)/shard_map/ppermute | solution.py:22
  41.3 1.6 collective-permute-done.10
  42.9 4.4 %collective-permute-start.11 = (f32[32,256]{1,0:T(8,128)S(1)}, f32[32,256]{1,0:T(8,128)S(1)}, u32[]{:S(2)}, u32[]{:S(2)}) collective-permute-start(f32[32,256]{1,0:T(8,128)S(1)} %collective-permute-done.10), channel_id=1, source_target_pairs={{2,0},{4,2},{6,4},{8,6},{10,8},{12,10},{14,12},{16,14},{18,16},{20... | collective-permute-start | bytes 98312 | tf_op jit(solution)/shard_map/ppermute | solution.py:22
  47.4 1.6 collective-permute-done.11
  48.9 4.4 %collective-permute-start.12 = (f32[32,256]{1,0:T(8,128)S(1)}, f32[32,256]{1,0:T(8,128)S(1)}, u32[]{:S(2)}, u32[]{:S(2)}) collective-permute-start(f32[32,256]{1,0:T(8,128)S(1)} %collective-permute-done.11), channel_id=1, source_target_pairs={{2,0},{4,2},{6,4},{8,6},{10,8},{12,10},{14,12},{16,14},{18,16},{20... | collective-permute-start | bytes 98312 | tf_op jit(solution)/shard_map/ppermute | solution.py:22
  53.4 1.6 collective-permute-done.12
  55.0 4.4 %collective-permute-start.13 = (f32[32,256]{1,0:T(8,128)S(1)}, f32[32,256]{1,0:T(8,128)S(1)}, u32[]{:S(2)}, u32[]{:S(2)}) collective-permute-start(f32[32,256]{1,0:T(8,128)S(1)} %collective-permute-done.12), channel_id=1, source_target_pairs={{2,0},{4,2},{6,4},{8,6},{10,8},{12,10},{14,12},{16,14},{18,16},{20... | collective-permute-start | bytes 98312 | tf_op jit(solution)/shard_map/ppermute | solution.py:22
  59.5 19.4 %all_gather.6 = f32[32,4096]{1,0:T(8,128)S(1)} all-gather(f32[32,256]{1,0:T(8,128)S(1)} %bitcast.93), channel_id=1, replica_groups=mesh['blk'=16,'col'=2] {'blk'}, dimensions={1}, use_global_device_ids=true | all-gather | bytes 557056 | tf_op jit(solution)/shard_map/all_gather | solution.py:75
  79.1 1.2 collective-permute-start.14
  80.5 1.4 collective-permute-done.14
  81.9 0.6 gather_fusion
  82.5 30.2 %while.11 = (s32[]{:T(128)}, f32[32,512]{1,0:T(8,128)S(1)}, f32[16,32,256]{2,0,1:T(8,128)S(1)}, f32[]{:T(128)}, f32[512]{0:T(512)S(1)}, /*index=5*/f32[16,32,256...) while((s32[]{:T(128)}, f32[32,512]{1,0:T(8,128)S(1)}, f32[16,32,256]{2,0,1:T(8,128)S(1)}, ...), condition=%wide.region_5.6_spmd.clone, body=%wide.region_3.5_spmd.clone.sunk | while | flops 101367552 | bytes 1413239 | solution.py:70
  82.5 1.4 fusion.30
  84.0 0.4 convolution_add_fusion.2
  84.4 1.4 fusion.30
  85.8 0.4 convolution_add_fusion.2
  86.3 1.4 fusion.30
  87.7 0.4 convolution_add_fusion.2
  88.2 1.4 fusion.30
  89.6 0.4 convolution_add_fusion.2
  90.1 1.4 fusion.30
  92.0 1.4 fusion.30
  93.9 1.4 fusion.30
  95.7 1.4 fusion.30
  97.6 1.4 fusion.30
  99.5 1.4 fusion.30
  101.4 1.4 fusion.30
  103.3 1.4 fusion.30
  105.2 1.4 fusion.30
  107.1 1.4 fusion.30
  108.9 1.4 fusion.30
  110.8 1.4 fusion.30
  112.7 0.6 copy-done.1
  114.0 11.0 %reduce-scatter.2.cloned.1.call-done = f32[16,512]{1,0:T(8,128)} async-done(((f32[32,512]{1,0:T(8,128)}), f32[16,512]{1,0:T(8,128)}) %reduce-scatter.2.cloned.1.call-update) | async-done | bytes 32784 | tf_op jit(solution)/shard_map/reduce_scatter | solution.py:78
  125.0 0.9 multiply_reduce_fusion.1
  125.9 32.6 %all-reduce = (f32[16]{0:T(128)S(1)}, f32[16]{0:T(128)S(1)}) all-reduce(f32[16]{0:T(128)S(1)} %get-tuple-element.86, f32[16]{0:T(128)S(1)} %get-tuple-element.85), channel_id=1, replica_groups=mesh['blk'=16,'col'=2] {'blk'}, use_global_device_ids=true, to_apply=%region_1.0 | all-reduce | flops 32 | bytes 256 | tf_op jit(solution)/shard_map/psum | solution.py:30
  158.5 0.7 multiply_subtract_fusion
  (90 shorter events, 6.4 us)
Async XLA Ops:
  7.2 1.2 copy-start
  7.2 22.1 %copy-start.2 = (f32[16,512]{1,0:T(8,128)S(1)}, f32[16,512]{1,0:T(8,128)}, u32[]{:S(2)}) copy-start(f32[16,512]{1,0:T(8,128)} %param.15) | copy-start | bytes 98308
  10.0 7.1 %collective-permute-start = (f32[32,256]{1,0:T(8,128)S(1)}, f32[32,256]{1,0:T(8,128)S(1)}, u32[]{:S(2)}, u32[]{:S(2)}) collective-permute-start(f32[32,256]{1,0:T(8,128)S(1)} %bitcast.90), channel_id=1, source_target_pairs={{0,2},{2,4},{4,6},{6,8},{8,10},{10,12},{12,14},{14,16},{16,18},{18... | collective-permute-start | bytes 98312 | tf_op jit(solution)/shard_map/ppermute | solution.py:20
  17.2 6.0 %collective-permute-start.1 = (f32[32,256]{1,0:T(8,128)S(1)}, f32[32,256]{1,0:T(8,128)S(1)}, u32[]{:S(2)}, u32[]{:S(2)}) collective-permute-start(f32[32,256]{1,0:T(8,128)S(1)} %collective-permute-done), channel_id=1, source_target_pairs={{0,2},{2,4},{4,6},{6,8},{8,10},{10,12},{12,14},{14,16},{16,18},{18... | collective-permute-start | bytes 98312 | tf_op jit(solution)/shard_map/ppermute | solution.py:20
  17.2 6.1 %collective-permute-start.8 = (f32[32,256]{1,0:T(8,128)S(1)}, f32[32,256]{1,0:T(8,128)S(1)}, u32[]{:S(2)}, u32[]{:S(2)}) collective-permute-start(f32[32,256]{1,0:T(8,128)S(1)} %bitcast.91), channel_id=1, source_target_pairs={{2,0},{4,2},{6,4},{8,6},{10,8},{12,10},{14,12},{16,14},{18,16},{20... | collective-permute-start | bytes 98312 | tf_op jit(solution)/shard_map/ppermute | solution.py:22
  23.2 6.0 %collective-permute-start.2 = (f32[32,256]{1,0:T(8,128)S(1)}, f32[32,256]{1,0:T(8,128)S(1)}, u32[]{:S(2)}, u32[]{:S(2)}) collective-permute-start(f32[32,256]{1,0:T(8,128)S(1)} %collective-permute-done.1), channel_id=1, source_target_pairs={{0,2},{2,4},{4,6},{6,8},{8,10},{10,12},{12,14},{14,16},{16,18},{18... | collective-permute-start | bytes 98312 | tf_op jit(solution)/shard_map/ppermute | solution.py:20
  23.2 14.6 %collective-permute-start.9 = (f32[32,256]{1,0:T(8,128)S(1)}, f32[32,256]{1,0:T(8,128)S(1)}, u32[]{:S(2)}, u32[]{:S(2)}) collective-permute-start(f32[32,256]{1,0:T(8,128)S(1)} %collective-permute-done.8), channel_id=1, source_target_pairs={{2,0},{4,2},{6,4},{8,6},{10,8},{12,10},{14,12},{16,14},{18,16},{20... | collective-permute-start | bytes 98312 | tf_op jit(solution)/shard_map/ppermute | solution.py:22
  29.2 12.1 %collective-permute-start.3 = (f32[32,256]{1,0:T(8,128)S(1)}, f32[32,256]{1,0:T(8,128)S(1)}, u32[]{:S(2)}, u32[]{:S(2)}) collective-permute-start(f32[32,256]{1,0:T(8,128)S(1)} %collective-permute-done.2), channel_id=1, source_target_pairs={{0,2},{2,4},{4,6},{6,8},{8,10},{10,12},{12,14},{14,16},{16,18},{18... | collective-permute-start | bytes 98312 | tf_op jit(solution)/shard_map/ppermute | solution.py:20
  29.9 29.6 %all-to-all-start = ((f32[16,2,256]{2,0,1:T(8,128)}), f32[16,2,256]{2,0,1:T(8,128)S(1)}, u32[]{:S(2)}, u32[]{:S(2)}) async-start(f32[16,2,256]{2,0,1:T(8,128)} %bitcast.72), calls=%async_computation | async-start | bytes 65536 | tf_op jit(solution)/shard_map/all_to_all | solution.py:53
  33.1 91.8 %reduce-scatter.2.cloned.1.call-start = ((), (), s32[]{:S(2)}) async-start(), calls=%async_computation.2 | async-start | bytes 98304 | tf_op jit(solution)/shard_map/reduce_scatter | solution.py:78
  37.8 5.1 %collective-permute-start.10 = (f32[32,256]{1,0:T(8,128)S(1)}, f32[32,256]{1,0:T(8,128)S(1)}, u32[]{:S(2)}, u32[]{:S(2)}) collective-permute-start(f32[32,256]{1,0:T(8,128)S(1)} %collective-permute-done.9), channel_id=1, source_target_pairs={{2,0},{4,2},{6,4},{8,6},{10,8},{12,10},{14,12},{16,14},{18,16},{20... | collective-permute-start | bytes 98312 | tf_op jit(solution)/shard_map/ppermute | solution.py:22
  41.3 6.0 %collective-permute-start.4 = (f32[32,256]{1,0:T(8,128)S(1)}, f32[32,256]{1,0:T(8,128)S(1)}, u32[]{:S(2)}, u32[]{:S(2)}) collective-permute-start(f32[32,256]{1,0:T(8,128)S(1)} %collective-permute-done.3), channel_id=1, source_target_pairs={{0,2},{2,4},{4,6},{6,8},{8,10},{10,12},{12,14},{14,16},{16,18},{18... | collective-permute-start | bytes 98312 | tf_op jit(solution)/shard_map/ppermute | solution.py:20
  42.9 6.0 %collective-permute-start.11 = (f32[32,256]{1,0:T(8,128)S(1)}, f32[32,256]{1,0:T(8,128)S(1)}, u32[]{:S(2)}, u32[]{:S(2)}) collective-permute-start(f32[32,256]{1,0:T(8,128)S(1)} %collective-permute-done.10), channel_id=1, source_target_pairs={{2,0},{4,2},{6,4},{8,6},{10,8},{12,10},{14,12},{16,14},{18,16},{20... | collective-permute-start | bytes 98312 | tf_op jit(solution)/shard_map/ppermute | solution.py:22
  47.4 6.0 %collective-permute-start.5 = (f32[32,256]{1,0:T(8,128)S(1)}, f32[32,256]{1,0:T(8,128)S(1)}, u32[]{:S(2)}, u32[]{:S(2)}) collective-permute-start(f32[32,256]{1,0:T(8,128)S(1)} %collective-permute-done.4), channel_id=1, source_target_pairs={{0,2},{2,4},{4,6},{6,8},{8,10},{10,12},{12,14},{14,16},{16,18},{18... | collective-permute-start | bytes 98312 | tf_op jit(solution)/shard_map/ppermute | solution.py:20
  48.9 6.0 %collective-permute-start.12 = (f32[32,256]{1,0:T(8,128)S(1)}, f32[32,256]{1,0:T(8,128)S(1)}, u32[]{:S(2)}, u32[]{:S(2)}) collective-permute-start(f32[32,256]{1,0:T(8,128)S(1)} %collective-permute-done.11), channel_id=1, source_target_pairs={{2,0},{4,2},{6,4},{8,6},{10,8},{12,10},{14,12},{16,14},{18,16},{20... | collective-permute-start | bytes 98312 | tf_op jit(solution)/shard_map/ppermute | solution.py:22
  53.4 6.1 %collective-permute-start.6 = (f32[32,256]{1,0:T(8,128)S(1)}, f32[32,256]{1,0:T(8,128)S(1)}, u32[]{:S(2)}, u32[]{:S(2)}) collective-permute-start(f32[32,256]{1,0:T(8,128)S(1)} %collective-permute-done.5), channel_id=1, source_target_pairs={{0,2},{2,4},{4,6},{6,8},{8,10},{10,12},{12,14},{14,16},{16,18},{18... | collective-permute-start | bytes 98312 | tf_op jit(solution)/shard_map/ppermute | solution.py:20
  55.0 24.1 %collective-permute-start.13 = (f32[32,256]{1,0:T(8,128)S(1)}, f32[32,256]{1,0:T(8,128)S(1)}, u32[]{:S(2)}, u32[]{:S(2)}) collective-permute-start(f32[32,256]{1,0:T(8,128)S(1)} %collective-permute-done.12), channel_id=1, source_target_pairs={{2,0},{4,2},{6,4},{8,6},{10,8},{12,10},{14,12},{16,14},{18,16},{20... | collective-permute-start | bytes 98312 | tf_op jit(solution)/shard_map/ppermute | solution.py:22
  59.5 20.9 %collective-permute-start.7 = (f32[32,256]{1,0:T(8,128)S(1)}, f32[32,256]{1,0:T(8,128)S(1)}, u32[]{:S(2)}, u32[]{:S(2)}) collective-permute-start(f32[32,256]{1,0:T(8,128)S(1)} %collective-permute-done.6), channel_id=1, source_target_pairs={{0,2},{2,4},{4,6},{6,8},{8,10},{10,12},{12,14},{14,16},{16,18},{18... | collective-permute-start | bytes 98312 | tf_op jit(solution)/shard_map/ppermute | solution.py:20
  79.1 2.8 %collective-permute-start.14 = (f32[32,256]{1,0:T(8,128)S(1)}, f32[32,256]{1,0:T(8,128)S(1)}, u32[]{:S(2)}, u32[]{:S(2)}) collective-permute-start(f32[32,256]{1,0:T(8,128)S(1)} %collective-permute-done.13), channel_id=1, source_target_pairs={{2,0},{4,2},{6,4},{8,6},{10,8},{12,10},{14,12},{16,14},{18,16},{20... | collective-permute-start | bytes 98312 | tf_op jit(solution)/shard_map/ppermute | solution.py:22
  112.7 0.6 copy-start.1
  125.0 33.6 %copy-start.3 = (f32[16,512]{1,0:T(8,128)S(1)}, f32[16,512]{1,0:T(8,128)}, u32[]{:S(2)}) copy-start(f32[16,512]{1,0:T(8,128)} %reduce-scatter.2.cloned.1.call-done) | copy-start | bytes 98308
Sparse Core Ops, SparseCore 0:
  113.5 11.4 reduce-scatter.1
